TPU v7x, 32 devices: a whole 2x2x4 slice. The times are simulated.
32 devices in a mesh: gx: 8 (over y, x, core), gy: 4 (over z).
Axes of the slice: x: 2, y: 2, z: 4, core: 2. Of those that a mesh axis runs over, the one named last changes fastest.
Arguments:
- snapshots: bfloat16 [2, 1, 256, 256, 512], P(None, None, 'gx', 'gy'), may hold values from -12 to 12
- start: float32 [1, 32, 256, 256], P(None, None, 'gx', 'gy'), may hold values from -6 to 6
Outputs:
- basis_field: float32 [1, 32, 256, 256], P(None, None, 'gx', 'gy')
- phi: float32 [1, 2, 32, 32], replicated
All inputs are finite; a program needn't handle non-finite values.
Results may differ from a plain program's by a relative error of at most 0.0005.
Values may be sent and summed in bfloat16 or wider, within the bound.
A program may use at most 64 MiB of HBM per device.

v0:
```python
import jax
import jax.numpy as jnp
from jax import lax
from jax.sharding import PartitionSpec as P

ITERS = 4
precise = lax.Precision.HIGHEST


def swapped(x, axis, apart):
    return lax.ppermute(x, axis, [(i, i ^ 1 << apart) for i in range(lax.axis_size(axis))])


def passed_along(block, axis, distance):
    devices = range(lax.axis_size(axis))
    route = [(i - distance, i) for i in devices if i - distance in devices]
    return lax.ppermute(block, axis, route)


def inverse_factor(matrix):
    factor = jnp.linalg.cholesky(matrix)
    identity = jnp.broadcast_to(jnp.eye(matrix.shape[-1], dtype=matrix.dtype), matrix.shape)
    inverse = lax.linalg.triangular_solve(factor, identity, left_side=True, lower=True)
    return (factor, inverse)


def apply_inverse(inverse, right_side):
    return jnp.einsum("...kj,...jm->...km", inverse, right_side, precision=precise)


def shift_solve(inverse, right_matrix):
    inner = apply_inverse(inverse, right_matrix)
    return apply_inverse(jnp.swapaxes(inverse, -1, -2), inner)


def project(local_side):
    return lax.psum(local_side, ("gx", "gy"))


def gram_of(grown):
    return jnp.einsum("fkm,fjm->fkj", grown, grown, precision=precise)


def pair_grams(plus_terms, minus_terms):
    left_matrix = jnp.einsum("fkab,fjab->fkj", plus_terms, plus_terms, precision=precise)
    right_matrix = jnp.einsum("fkab,fjab->fkj", plus_terms, minus_terms, precision=precise)
    return (left_matrix, right_matrix)


def mirror_fields(stacked, rows, cols):
    moved = stacked
    for bit_number in range(lax.axis_size("gx").bit_length() - 1):
        moved = swapped(moved, "gx", bit_number)
    for bit_number in range(lax.axis_size("gy").bit_length() - 1):
        moved = swapped(moved, "gy", bit_number)
    lead = moved.shape[:-1]
    turned = moved.reshape(lead + (rows, cols))[..., ::-1, ::-1]
    return turned.reshape(moved.shape)


def shift_terms(field):
    rows = field.shape[2]
    cols = field.shape[3]
    below = passed_along(field[:, :, :1, :], "gx", -1)
    beside = passed_along(field[:, :, :, :1], "gy", -1)
    last_row_device = lax.axis_index("gx") == lax.axis_size("gx") - 1
    last_col_device = lax.axis_index("gy") == lax.axis_size("gy") - 1
    row_weight = jnp.where((jnp.arange(rows) == rows - 1) & last_row_device, 0.0, 1.0).astype(
        jnp.float32
    )
    col_weight = jnp.where((jnp.arange(cols) == cols - 1) & last_col_device, 0.0, 1.0).astype(
        jnp.float32
    )
    row_extended = jnp.concatenate([field, below], axis=2)
    col_extended = jnp.concatenate([field, beside], axis=3)
    row_plus = (row_extended[:, :, 1:] + row_extended[:, :, :-1]) * row_weight[:, None]
    row_minus = row_extended[:, :, 1:] - row_extended[:, :, :-1]
    col_plus = (col_extended[:, :, :, 1:] + col_extended[:, :, :, :-1]) * col_weight
    col_minus = col_extended[:, :, :, 1:] - col_extended[:, :, :, :-1]
    row_lhs, row_rhs = pair_grams(row_plus, row_minus)
    col_lhs, col_rhs = pair_grams(col_plus, col_minus)
    return (row_lhs, row_rhs, col_lhs, col_rhs)


def body(snapshots, start):
    frames, basis_count, rows, cols = start.shape
    upper_half = lax.axis_index("gx") < lax.axis_size("gx") // 2
    start_flat = start.reshape(frames, basis_count, rows * cols)
    own = snapshots.astype(jnp.float32).reshape(2, frames, rows * cols, -1)

    def local_side(weights, weights_mirror):
        p_real = jnp.einsum("fkm,fms->fks", weights, own[0], precision=precise)
        p_imag = jnp.einsum("fkm,fms->fks", weights, own[1], precision=precise)
        q_real = jnp.einsum("fkm,fms->fks", weights_mirror, own[0], precision=precise)
        q_imag = jnp.einsum("fkm,fms->fks", weights_mirror, own[1], precision=precise)
        first = jnp.where(upper_half, p_real - q_imag, p_imag + q_real)
        second = jnp.where(upper_half, -p_imag - q_real, p_real - q_imag)
        return jnp.concatenate([first, second], axis=-1)

    start_mirror = mirror_fields(start_flat[None], rows, cols)[0]
    basis = start_flat
    basis_mirror = start_mirror
    for step_index in range(ITERS):
        side = project(local_side(basis, basis_mirror))
        half = side.shape[-1] // 2
        side_first = side[..., :half]
        side_second = side[..., half:]
        g_real = jnp.einsum("fks,fms->fkm", side_first, own[0], precision=precise) - jnp.einsum(
            "fks,fms->fkm", side_second, own[1], precision=precise
        )
        g_imag = jnp.einsum("fks,fms->fkm", side_first, own[1], precision=precise) + jnp.einsum(
            "fks,fms->fkm", side_second, own[0], precision=precise
        )
        moved = mirror_fields(jnp.stack([g_real, g_imag]), rows, cols)
        grown = jnp.where(upper_half, g_real + moved[0], g_imag - moved[1])
        grown_mirror = jnp.where(upper_half, moved[1] - g_imag, moved[0] + g_real)
        grown, grown_mirror = (grown, grown_mirror)
        gram = lax.psum(gram_of(grown), ("gx", "gy"))
        factor, inverse = inverse_factor(gram)
        basis = apply_inverse(inverse, grown)
        basis_mirror = apply_inverse(inverse, grown_mirror)
    field = basis.reshape(frames, basis_count, rows, cols)
    local_terms = shift_terms(field)
    row_lhs, row_rhs, col_lhs, col_rhs = lax.psum(
        (local_terms[0], local_terms[1], local_terms[2], local_terms[3]), ("gx", "gy")
    )
    factors, inverses = inverse_factor(jnp.stack([row_lhs, col_lhs]))
    phi = jnp.swapaxes(shift_solve(inverses, jnp.stack([row_rhs, col_rhs])), 0, 1)
    return (field, phi)


def solution(mesh):
    return jax.shard_map(
        body,
        mesh=mesh,
        in_specs=(P(None, None, "gx", "gy", None), P(None, None, "gx", "gy")),
        out_specs=(P(None, None, "gx", "gy"), P()),
        check_vma=False,
    )
```

profile of v0, /device:TPU:0, one launch (start us, length us, event | category | flops | bytes accessed | tf_op | source)
XLA Modules:
  0.0 1151.4 jit_solution(10792632579092109949)
XLA Ops:
  10.2 2.8 collective-permute-start.1
  14.2 5.4 collective-permute-done.1
  21.4 2.6 fusion.107
  24.0 3.4 collective-permute-done.2
  30.0 4.3 collective-permute-done.3
  34.3 2.3 collective-permute-start.4
  37.7 9.2 collective-permute-done.4
  47.3 2.9 fusion.7
  50.2 2.9 select_bitcast_fusion.7
  53.8 125.0 %all-reduce.6.cloned.1.call-done = f32[1,32,1024]{2,1,0:T(8,128)} async-done(((f32[1,32,1024]{2,1,0:T(8,128)}), f32[1,32,1024]{2,1,0:T(8,128)}) %all-reduce.6.cloned.1.call-update) | async-done | bytes 131088 | tf_op jit(solution)/shard_map/psum | solution.py:37
  178.9 2.9 fusion.52
  181.8 1.9 fusion.51
  183.7 1.9 convolution_subtract_fusion.3
  185.6 1.9 convolution_add_fusion.3
  187.6 1.9 collective-permute-done.5
  191.0 12.5 %collective-permute-done.6 = f32[2,1,32,2048]{3,2,1,0:T(8,128)S(1)} collective-permute-done((f32[2,1,32,2048]{3,2,1,0:T(8,128)S(1)}, f32[2,1,32,2048]{3,2,1,0:T(8,128)S(1)}, u32[]{:S(2)}, u32[]{:S(2)}) %collective-permute-start.6) | collective-permute-done | bytes 524320 | tf_op jit(solution)/shard_map/ppermute | solution.py:11
  204.9 11.6 %collective-permute-done.7 = f32[2,1,32,2048]{3,2,1,0:T(8,128)S(1)} collective-permute-done((f32[2,1,32,2048]{3,2,1,0:T(8,128)S(1)}, f32[2,1,32,2048]{3,2,1,0:T(8,128)S(1)}, u32[]{:S(2)}, u32[]{:S(2)}) %collective-permute-start.7) | collective-permute-done | bytes 524320 | tf_op jit(solution)/shard_map/ppermute | solution.py:11
  218.0 10.8 collective-permute-done.8
  230.3 22.1 %collective-permute-done.9 = f32[2,1,32,2048]{3,2,1,0:T(8,128)S(1)} collective-permute-done((f32[2,1,32,2048]{3,2,1,0:T(8,128)S(1)}, f32[2,1,32,2048]{3,2,1,0:T(8,128)S(1)}, u32[]{:S(2)}, u32[]{:S(2)}) %collective-permute-start.9) | collective-permute-done | bytes 524320 | tf_op jit(solution)/shard_map/ppermute | solution.py:11
  259.4 38.0 %psum.85 = f32[1,32,32]{1,2,0:T(8,128)S(1)} all-reduce(f32[1,32,32]{1,2,0:T(8,128)S(1)} %convolution_bitcast_fusion.10), channel_id=1, replica_groups=mesh['gx'=8,'gy'=4] {'gx','gy'}, use_global_device_ids=true, to_apply=%region_1.2 | all-reduce | flops 1024 | bytes 8192 | tf_op jit(solution)/shard_map/psum | solution.py:118
  297.4 2.9 custom-call.21
  301.7 2.4 custom-call.22
  310.2 125.8 %all-reduce.8.cloned.1.call-done = f32[1,32,1024]{2,1,0:T(8,128)} async-done(((f32[1,32,1024]{2,1,0:T(8,128)}), f32[1,32,1024]{2,1,0:T(8,128)}) %all-reduce.8.cloned.1.call-update) | async-done | bytes 131088 | tf_op jit(solution)/shard_map/psum | solution.py:37
  436.1 2.9 fusion.54
  439.0 1.9 fusion.53
  440.9 1.9 convolution_subtract_fusion.2
  442.8 1.9 convolution_add_fusion.2
  444.8 1.9 collective-permute-done.10
  448.2 12.5 %collective-permute-done.11 = f32[2,1,32,2048]{3,2,1,0:T(8,128)S(1)} collective-permute-done((f32[2,1,32,2048]{3,2,1,0:T(8,128)S(1)}, f32[2,1,32,2048]{3,2,1,0:T(8,128)S(1)}, u32[]{:S(2)}, u32[]{:S(2)}) %collective-permute-start.11) | collective-permute-done | bytes 524320 | tf_op jit(solution)/shard_map/ppermute | solution.py:11
  462.1 11.6 %collective-permute-done.12 = f32[2,1,32,2048]{3,2,1,0:T(8,128)S(1)} collective-permute-done((f32[2,1,32,2048]{3,2,1,0:T(8,128)S(1)}, f32[2,1,32,2048]{3,2,1,0:T(8,128)S(1)}, u32[]{:S(2)}, u32[]{:S(2)}) %collective-permute-start.12) | collective-permute-done | bytes 524320 | tf_op jit(solution)/shard_map/ppermute | solution.py:11
  475.3 10.8 collective-permute-done.13
  487.5 22.1 %collective-permute-done.14 = f32[2,1,32,2048]{3,2,1,0:T(8,128)S(1)} collective-permute-done((f32[2,1,32,2048]{3,2,1,0:T(8,128)S(1)}, f32[2,1,32,2048]{3,2,1,0:T(8,128)S(1)}, u32[]{:S(2)}, u32[]{:S(2)}) %collective-permute-start.14) | collective-permute-done | bytes 524320 | tf_op jit(solution)/shard_map/ppermute | solution.py:11
  516.6 38.1 %psum.87 = f32[1,32,32]{1,2,0:T(8,128)S(1)} all-reduce(f32[1,32,32]{1,2,0:T(8,128)S(1)} %convolution_bitcast_fusion.9), channel_id=1, replica_groups=mesh['gx'=8,'gy'=4] {'gx','gy'}, use_global_device_ids=true, to_apply=%region_5.8 | all-reduce | flops 1024 | bytes 8192 | tf_op jit(solution)/shard_map/psum | solution.py:118
  554.7 2.9 custom-call.23
  559.0 2.4 custom-call.24
  567.5 125.8 %all-reduce.10.cloned.1.call-done = f32[1,32,1024]{2,1,0:T(8,128)} async-done(((f32[1,32,1024]{2,1,0:T(8,128)}), f32[1,32,1024]{2,1,0:T(8,128)}) %all-reduce.10.cloned.1.call-update) | async-done | bytes 131088 | tf_op jit(solution)/shard_map/psum | solution.py:37
  693.3 2.9 fusion.56
  696.2 1.9 fusion.55
  698.1 1.9 convolution_subtract_fusion.1
  700.0 1.9 convolution_add_fusion.1
  702.0 1.9 collective-permute-done.15
  705.4 12.5 %collective-permute-done.16 = f32[2,1,32,2048]{3,2,1,0:T(8,128)S(1)} collective-permute-done((f32[2,1,32,2048]{3,2,1,0:T(8,128)S(1)}, f32[2,1,32,2048]{3,2,1,0:T(8,128)S(1)}, u32[]{:S(2)}, u32[]{:S(2)}) %collective-permute-start.16) | collective-permute-done | bytes 524320 | tf_op jit(solution)/shard_map/ppermute | solution.py:11
  719.4 11.6 %collective-permute-done.17 = f32[2,1,32,2048]{3,2,1,0:T(8,128)S(1)} collective-permute-done((f32[2,1,32,2048]{3,2,1,0:T(8,128)S(1)}, f32[2,1,32,2048]{3,2,1,0:T(8,128)S(1)}, u32[]{:S(2)}, u32[]{:S(2)}) %collective-permute-start.17) | collective-permute-done | bytes 524320 | tf_op jit(solution)/shard_map/ppermute | solution.py:11
  732.5 10.8 collective-permute-done.18
  744.7 22.1 %collective-permute-done.19 = f32[2,1,32,2048]{3,2,1,0:T(8,128)S(1)} collective-permute-done((f32[2,1,32,2048]{3,2,1,0:T(8,128)S(1)}, f32[2,1,32,2048]{3,2,1,0:T(8,128)S(1)}, u32[]{:S(2)}, u32[]{:S(2)}) %collective-permute-start.19) | collective-permute-done | bytes 524320 | tf_op jit(solution)/shard_map/ppermute | solution.py:11
  773.8 38.2 %psum.89 = f32[1,32,32]{1,2,0:T(8,128)S(1)} all-reduce(f32[1,32,32]{1,2,0:T(8,128)S(1)} %convolution_bitcast_fusion.8), channel_id=1, replica_groups=mesh['gx'=8,'gy'=4] {'gx','gy'}, use_global_device_ids=true, to_apply=%region_7.10 | all-reduce | flops 1024 | bytes 8192 | tf_op jit(solution)/shard_map/psum | solution.py:118
  812.1 2.9 custom-call.25
  816.4 2.4 custom-call.26
  824.9 125.8 %all-reduce.12.cloned.1.call-done = f32[1,32,1024]{2,1,0:T(8,128)} async-done(((f32[1,32,1024]{2,1,0:T(8,128)}), f32[1,32,1024]{2,1,0:T(8,128)}) %all-reduce.12.cloned.1.call-update) | async-done | bytes 131088 | tf_op jit(solution)/shard_map/psum | solution.py:37
  950.7 2.9 fusion.58
  955.5 1.9 convolution_subtract_fusion
  957.4 1.9 convolution_add_fusion
  959.5 1.9 collective-permute-done.20
  962.8 12.5 %collective-permute-done.21 = f32[2,1,32,2048]{3,2,1,0:T(8,128)S(1)} collective-permute-done((f32[2,1,32,2048]{3,2,1,0:T(8,128)S(1)}, f32[2,1,32,2048]{3,2,1,0:T(8,128)S(1)}, u32[]{:S(2)}, u32[]{:S(2)}) %collective-permute-start.21) | collective-permute-done | bytes 524320 | tf_op jit(solution)/shard_map/ppermute | solution.py:11
  976.8 11.6 %collective-permute-done.22 = f32[2,1,32,2048]{3,2,1,0:T(8,128)S(1)} collective-permute-done((f32[2,1,32,2048]{3,2,1,0:T(8,128)S(1)}, f32[2,1,32,2048]{3,2,1,0:T(8,128)S(1)}, u32[]{:S(2)}, u32[]{:S(2)}) %collective-permute-start.22) | collective-permute-done | bytes 524320 | tf_op jit(solution)/shard_map/ppermute | solution.py:11
  989.9 10.8 collective-permute-done.23
  1002.2 22.0 %collective-permute-done.24 = f32[2,1,32,2048]{3,2,1,0:T(8,128)S(1)} collective-permute-done((f32[2,1,32,2048]{3,2,1,0:T(8,128)S(1)}, f32[2,1,32,2048]{3,2,1,0:T(8,128)S(1)}, u32[]{:S(2)}, u32[]{:S(2)}) %collective-permute-start.24) | collective-permute-done | bytes 524320 | tf_op jit(solution)/shard_map/ppermute | solution.py:11
  1026.1 38.0 %psum.91 = f32[1,32,32]{1,2,0:T(8,128)S(1)} all-reduce(f32[1,32,32]{1,2,0:T(8,128)S(1)} %convolution_bitcast_fusion.7), channel_id=1, replica_groups=mesh['gx'=8,'gy'=4] {'gx','gy'}, use_global_device_ids=true, to_apply=%region_9.12 | all-reduce | flops 1024 | bytes 8192 | tf_op jit(solution)/shard_map/psum | solution.py:118
  1064.2 2.9 custom-call.27
  1068.5 2.4 custom-call.28
  1075.8 12.2 %collective-permute-done.26 = f32[1,32,32,1]{3,1,2,0:T(8,128)S(1)} collective-permute-done((f32[1,32,32,1]{3,1,2,0:T(8,128)S(1)}, f32[1,32,32,1]{3,1,2,0:T(8,128)S(1)}, u32[]{:S(2)}, u32[]{:S(2)}) %collective-permute-start.26) | collective-permute-done | bytes 4128 | tf_op jit(solution)/shard_map/ppermute | solution.py:17
  1091.3 40.9 %all-reduce = (f32[1,1,32,32]{2,3,1,0:T(8,128)S(1)}, f32[1,1,32,32]{2,3,1,0:T(8,128)S(1)}, f32[1,1,32,32]{3,2,1,0:T(8,128)S(1)}, f32[1,1,32,32]{3,2,1,0:T(8,128)S(1)}) all-reduce(f32[1,1,32,32]{2,3,1,0:T(8,128)S(1)} %convolution_bitcast_fusion.5, ...), channel_id=1, replica_groups=mesh['gx'=8,'gy'=4] {'gx','gy'}, use_global_device_ids=true, to_apply=%region_10.13 | all-reduce | flops 4096 | bytes 32768 | tf_op jit(solution)/shard_map/psum | solution.py:124
  1132.4 5.9 custom-call.13
  1138.5 4.9 custom-call.14
  (175 shorter events, 93.0 us)
Async XLA Ops:
  7.2 171.7 %all-reduce.6.cloned.1.call-start = ((), (), s32[]{:S(2)}) async-start(), calls=%async_computation | async-start | bytes 262144 | tf_op jit(solution)/shard_map/psum | solution.py:37
  8.4 1.7 collective-permute-start
  10.2 9.5 collective-permute-start.1
  19.6 7.8 collective-permute-start.2
  24.0 13.7 %copy-start = (bf16[1,1,32,64,512]{4,3,2,1,0:T(8,128)(2,1)}, bf16[1,1,32,64,512]{4,3,2,1,0:T(8,128)(2,1)S(1)}, u32[]{:S(2)}) copy-start(bf16[1,1,32,64,512]{4,3,2,1,0:T(8,128)(2,1)S(1)} %get-tuple-element.15) | copy-start | bytes 6291460
  27.4 6.9 collective-permute-start.3
  34.3 12.6 %collective-permute-start.4 = (f32[1,1,32,2048]{3,2,1,0:T(8,128)S(1)}, f32[1,1,32,2048]{3,2,1,0:T(8,128)S(1)}, u32[]{:S(2)}, u32[]{:S(2)}) collective-permute-start(f32[1,1,32,2048]{3,2,1,0:T(8,128)S(1)} %collective-permute-done.3), channel_id=1, source_target_pairs={{0,2},{1,3},{2,0},{3,1},{4,6},{5,7},{6,4},{7,5},{8,10},{9,11},{10,... | collective-permute-start | bytes 786440 | tf_op jit(solution)/shard_map/ppermute | solution.py:11
  53.8 382.3 %all-reduce.8.cloned.1.call-start = ((), (), s32[]{:S(2)}) async-start(), calls=%async_computation.1 | async-start | bytes 262144 | tf_op jit(solution)/shard_map/psum | solution.py:37
  178.9 2.9 copy-start.1
  178.9 2.9 copy-start.8
  187.5 2.0 collective-permute-start.5
  189.5 14.0 %collective-permute-start.6 = (f32[2,1,32,2048]{3,2,1,0:T(8,128)S(1)}, f32[2,1,32,2048]{3,2,1,0:T(8,128)S(1)}, u32[]{:S(2)}, u32[]{:S(2)}) collective-permute-start(f32[2,1,32,2048]{3,2,1,0:T(8,128)S(1)} %collective-permute-done.5), channel_id=1, source_target_pairs={{0,8},{4,12},{8,0},{12,4},{16,24},{20,28},{24,16},{28,20},{1,9},{5... | collective-permute-start | bytes 1572872 | tf_op jit(solution)/shard_map/ppermute | solution.py:11
  203.5 13.1 %collective-permute-start.7 = (f32[2,1,32,2048]{3,2,1,0:T(8,128)S(1)}, f32[2,1,32,2048]{3,2,1,0:T(8,128)S(1)}, u32[]{:S(2)}, u32[]{:S(2)}) collective-permute-start(f32[2,1,32,2048]{3,2,1,0:T(8,128)S(1)} %collective-permute-done.6), channel_id=1, source_target_pairs={{0,16},{4,20},{8,24},{12,28},{16,0},{20,4},{24,8},{28,12},{1,17},{... | collective-permute-start | bytes 1572872 | tf_op jit(solution)/shard_map/ppermute | solution.py:11
  216.6 12.3 %collective-permute-start.8 = (f32[2,1,32,2048]{3,2,1,0:T(8,128)S(1)}, f32[2,1,32,2048]{3,2,1,0:T(8,128)S(1)}, u32[]{:S(2)}, u32[]{:S(2)}) collective-permute-start(f32[2,1,32,2048]{3,2,1,0:T(8,128)S(1)} %collective-permute-done.7), channel_id=1, source_target_pairs={{0,1},{1,0},{2,3},{3,2},{4,5},{5,4},{6,7},{7,6},{8,9},{9,8},{10,11... | collective-permute-start | bytes 1572872 | tf_op jit(solution)/shard_map/ppermute | solution.py:11
  228.8 23.5 %collective-permute-start.9 = (f32[2,1,32,2048]{3,2,1,0:T(8,128)S(1)}, f32[2,1,32,2048]{3,2,1,0:T(8,128)S(1)}, u32[]{:S(2)}, u32[]{:S(2)}) collective-permute-start(f32[2,1,32,2048]{3,2,1,0:T(8,128)S(1)} %collective-permute-done.8), channel_id=1, source_target_pairs={{0,2},{1,3},{2,0},{3,1},{4,6},{5,7},{6,4},{7,5},{8,10},{9,11},{10,... | collective-permute-start | bytes 1572872 | tf_op jit(solution)/shard_map/ppermute | solution.py:11
  304.4 1.8 copy-start.2
  310.2 383.1 %all-reduce.10.cloned.1.call-start = ((), (), s32[]{:S(2)}) async-start(), calls=%async_computation.2 | async-start | bytes 262144 | tf_op jit(solution)/shard_map/psum | solution.py:37
  436.1 2.9 copy-start.3
  436.1 2.9 copy-start.9
  444.7 2.0 collective-permute-start.10
  446.7 14.0 %collective-permute-start.11 = (f32[2,1,32,2048]{3,2,1,0:T(8,128)S(1)}, f32[2,1,32,2048]{3,2,1,0:T(8,128)S(1)}, u32[]{:S(2)}, u32[]{:S(2)}) collective-permute-start(f32[2,1,32,2048]{3,2,1,0:T(8,128)S(1)} %collective-permute-done.10), channel_id=1, source_target_pairs={{0,8},{4,12},{8,0},{12,4},{16,24},{20,28},{24,16},{28,20},{1,9},{5... | collective-permute-start | bytes 1572872 | tf_op jit(solution)/shard_map/ppermute | solution.py:11
  460.7 13.1 %collective-permute-start.12 = (f32[2,1,32,2048]{3,2,1,0:T(8,128)S(1)}, f32[2,1,32,2048]{3,2,1,0:T(8,128)S(1)}, u32[]{:S(2)}, u32[]{:S(2)}) collective-permute-start(f32[2,1,32,2048]{3,2,1,0:T(8,128)S(1)} %collective-permute-done.11), channel_id=1, source_target_pairs={{0,16},{4,20},{8,24},{12,28},{16,0},{20,4},{24,8},{28,12},{1,17},{... | collective-permute-start | bytes 1572872 | tf_op jit(solution)/shard_map/ppermute | solution.py:11
  473.8 12.3 %collective-permute-start.13 = (f32[2,1,32,2048]{3,2,1,0:T(8,128)S(1)}, f32[2,1,32,2048]{3,2,1,0:T(8,128)S(1)}, u32[]{:S(2)}, u32[]{:S(2)}) collective-permute-start(f32[2,1,32,2048]{3,2,1,0:T(8,128)S(1)} %collective-permute-done.12), channel_id=1, source_target_pairs={{0,1},{1,0},{2,3},{3,2},{4,5},{5,4},{6,7},{7,6},{8,9},{9,8},{10,11... | collective-permute-start | bytes 1572872 | tf_op jit(solution)/shard_map/ppermute | solution.py:11
  486.0 23.5 %collective-permute-start.14 = (f32[2,1,32,2048]{3,2,1,0:T(8,128)S(1)}, f32[2,1,32,2048]{3,2,1,0:T(8,128)S(1)}, u32[]{:S(2)}, u32[]{:S(2)}) collective-permute-start(f32[2,1,32,2048]{3,2,1,0:T(8,128)S(1)} %collective-permute-done.13), channel_id=1, source_target_pairs={{0,2},{1,3},{2,0},{3,1},{4,6},{5,7},{6,4},{7,5},{8,10},{9,11},{10,... | collective-permute-start | bytes 1572872 | tf_op jit(solution)/shard_map/ppermute | solution.py:11
  561.6 1.8 copy-start.4
  567.5 383.3 %all-reduce.12.cloned.1.call-start = ((), (), s32[]{:S(2)}) async-start(), calls=%async_computation.3 | async-start | bytes 262144 | tf_op jit(solution)/shard_map/psum | solution.py:37
  693.3 2.9 copy-start.5
  693.3 2.9 copy-start.10
  702.0 2.0 collective-permute-start.15
  703.9 14.0 %collective-permute-start.16 = (f32[2,1,32,2048]{3,2,1,0:T(8,128)S(1)}, f32[2,1,32,2048]{3,2,1,0:T(8,128)S(1)}, u32[]{:S(2)}, u32[]{:S(2)}) collective-permute-start(f32[2,1,32,2048]{3,2,1,0:T(8,128)S(1)} %collective-permute-done.15), channel_id=1, source_target_pairs={{0,8},{4,12},{8,0},{12,4},{16,24},{20,28},{24,16},{28,20},{1,9},{5... | collective-permute-start | bytes 1572872 | tf_op jit(solution)/shard_map/ppermute | solution.py:11
  717.9 13.1 %collective-permute-start.17 = (f32[2,1,32,2048]{3,2,1,0:T(8,128)S(1)}, f32[2,1,32,2048]{3,2,1,0:T(8,128)S(1)}, u32[]{:S(2)}, u32[]{:S(2)}) collective-permute-start(f32[2,1,32,2048]{3,2,1,0:T(8,128)S(1)} %collective-permute-done.16), channel_id=1, source_target_pairs={{0,16},{4,20},{8,24},{12,28},{16,0},{20,4},{24,8},{28,12},{1,17},{... | collective-permute-start | bytes 1572872 | tf_op jit(solution)/shard_map/ppermute | solution.py:11
  731.0 12.3 %collective-permute-start.18 = (f32[2,1,32,2048]{3,2,1,0:T(8,128)S(1)}, f32[2,1,32,2048]{3,2,1,0:T(8,128)S(1)}, u32[]{:S(2)}, u32[]{:S(2)}) collective-permute-start(f32[2,1,32,2048]{3,2,1,0:T(8,128)S(1)} %collective-permute-done.17), channel_id=1, source_target_pairs={{0,1},{1,0},{2,3},{3,2},{4,5},{5,4},{6,7},{7,6},{8,9},{9,8},{10,11... | collective-permute-start | bytes 1572872 | tf_op jit(solution)/shard_map/ppermute | solution.py:11
  743.3 23.5 %collective-permute-start.19 = (f32[2,1,32,2048]{3,2,1,0:T(8,128)S(1)}, f32[2,1,32,2048]{3,2,1,0:T(8,128)S(1)}, u32[]{:S(2)}, u32[]{:S(2)}) collective-permute-start(f32[2,1,32,2048]{3,2,1,0:T(8,128)S(1)} %collective-permute-done.18), channel_id=1, source_target_pairs={{0,2},{1,3},{2,0},{3,1},{4,6},{5,7},{6,4},{7,5},{8,10},{9,11},{10,... | collective-permute-start | bytes 1572872 | tf_op jit(solution)/shard_map/ppermute | solution.py:11
  819.1 1.8 copy-start.6
  950.7 2.9 copy-start.7
  950.7 2.9 copy-start.11
  959.4 2.0 collective-permute-start.20
  961.4 14.0 %collective-permute-start.21 = (f32[2,1,32,2048]{3,2,1,0:T(8,128)S(1)}, f32[2,1,32,2048]{3,2,1,0:T(8,128)S(1)}, u32[]{:S(2)}, u32[]{:S(2)}) collective-permute-start(f32[2,1,32,2048]{3,2,1,0:T(8,128)S(1)} %collective-permute-done.20), channel_id=1, source_target_pairs={{0,8},{4,12},{8,0},{12,4},{16,24},{20,28},{24,16},{28,20},{1,9},{5... | collective-permute-start | bytes 1572872 | tf_op jit(solution)/shard_map/ppermute | solution.py:11
  975.3 13.1 %collective-permute-start.22 = (f32[2,1,32,2048]{3,2,1,0:T(8,128)S(1)}, f32[2,1,32,2048]{3,2,1,0:T(8,128)S(1)}, u32[]{:S(2)}, u32[]{:S(2)}) collective-permute-start(f32[2,1,32,2048]{3,2,1,0:T(8,128)S(1)} %collective-permute-done.21), channel_id=1, source_target_pairs={{0,16},{4,20},{8,24},{12,28},{16,0},{20,4},{24,8},{28,12},{1,17},{... | collective-permute-start | bytes 1572872 | tf_op jit(solution)/shard_map/ppermute | solution.py:11
  988.4 12.3 %collective-permute-start.23 = (f32[2,1,32,2048]{3,2,1,0:T(8,128)S(1)}, f32[2,1,32,2048]{3,2,1,0:T(8,128)S(1)}, u32[]{:S(2)}, u32[]{:S(2)}) collective-permute-start(f32[2,1,32,2048]{3,2,1,0:T(8,128)S(1)} %collective-permute-done.22), channel_id=1, source_target_pairs={{0,1},{1,0},{2,3},{3,2},{4,5},{5,4},{6,7},{7,6},{8,9},{9,8},{10,11... | collective-permute-start | bytes 1572872 | tf_op jit(solution)/shard_map/ppermute | solution.py:11
  1000.7 23.5 %collective-permute-start.24 = (f32[2,1,32,2048]{3,2,1,0:T(8,128)S(1)}, f32[2,1,32,2048]{3,2,1,0:T(8,128)S(1)}, u32[]{:S(2)}, u32[]{:S(2)}) collective-permute-start(f32[2,1,32,2048]{3,2,1,0:T(8,128)S(1)} %collective-permute-done.23), channel_id=1, source_target_pairs={{0,2},{1,3},{2,0},{3,1},{4,6},{5,7},{6,4},{7,5},{8,10},{9,11},{10,... | collective-permute-start | bytes 1572872 | tf_op jit(solution)/shard_map/ppermute | solution.py:11
  1072.0 15.9 %collective-permute-start.26 = (f32[1,32,32,1]{3,1,2,0:T(8,128)S(1)}, f32[1,32,32,1]{3,1,2,0:T(8,128)S(1)}, u32[]{:S(2)}, u32[]{:S(2)}) collective-permute-start(f32[1,32,32,1]{3,1,2,0:T(8,128)S(1)} %bitcast.338), channel_id=1, source_target_pairs={{1,0},{2,1},{3,2},{5,4},{6,5},{7,6},{9,8},{10,9},{11,10},{13,12},{... | collective-permute-start | bytes 12296 | tf_op jit(solution)/shard_map/ppermute | solution.py:17
  1074.5 15.5 %collective-permute-start.25 = (f32[1,32,1,64]{3,1,2,0:T(8,128)S(1)}, f32[1,32,1,64]{3,1,2,0:T(8,128)S(1)}, u32[]{:S(2)}, u32[]{:S(2)}) collective-permute-start(f32[1,32,1,64]{3,1,2,0:T(8,128)S(1)} %slice.232), channel_id=1, source_target_pairs={{4,0},{8,4},{12,8},{16,12},{20,16},{24,20},{28,24},{5,1},{9,5},{13... | collective-permute-start | bytes 24584 | tf_op jit(solution)/shard_map/ppermute | solution.py:17
Sparse Core Ops, SparseCore 0:
  53.9 124.9 all-reduce.5
  310.3 125.6 all-reduce.7
  567.6 125.6 all-reduce.9
  825.0 125.6 all-reduce.11
where the time goes:
time: 1160 us; the launch traced here: 1150 us
  waiting for transfers between devices  774 us (67%)
  blocking collectives  193 us (17%)
  matrix products  65.3 us (6%)
  other arithmetic  40.8 us (4%)
  starting transfers between devices  35.6 us (3%)
  local copies, waits for them, and re-layouts  28.2 us (2%)
  between operations  14.8 us (1%)
    psum x4, waiting for transfers between devices, project(): return lax.psum(local_side, ('gx', 'gy'))  502 us
    ppermute x25, waiting for transfers between devices, swapped(): lax.ppermute(x, axis, [(i, i ^ 1 << apart) for i in range(lax.axis_size(a...  259 us
    psum x4, blocking collectives, body(): gram = lax.psum(gram_of(grown), ('gx', 'gy'))  152 us
    psum x1, blocking collectives, body(): lax.psum((local_terms[0], local_terms[1], local_terms[2], local_terms[3])...  40.9 us
    ppermute x25, starting transfers between devices, swapped(): lax.ppermute(x, axis, [(i, i ^ 1 << apart) for i in range(lax.axis_size(a...  32.9 us
  transfers between devices with their start and end apart: 31, of which 30 were waited for; matrix products, arithmetic and copies ran while one was open for 1% of the time, Pallas kernels for 0%

commit v1 on v0

--- a/solution.py
+++ b/solution.py
@@ -1,3 +1,4 @@
+import functools
 import jax
 import jax.numpy as jnp
 from jax import lax
@@ -5,6 +6,13 @@
 
 ITERS = 4
 precise = lax.Precision.HIGHEST
+
+
+def ways_resolve(row_data, across):
+    return jnp.sum(lax.all_gather(row_data, across), 0)
+
+
+shifts_all_draft = functools.partial(ways_resolve, across=("gx", "gy"))
 
 
 def swapped(x, axis, apart):
@@ -34,7 +42,7 @@
 
 
 def project(local_side):
-    return lax.psum(local_side, ("gx", "gy"))
+    return shifts_all_draft(local_side)
 
 
 def gram_of(grown):

time: 1160 us -> 920 us (0.79)
  waiting for transfers between devices: 774 us -> 523 us
    psum x4 -> x0, waiting for transfers between devices: 502 us -> none  [project(): return lax.psum(local_side, ('gx', 'gy'))]
    all_gather x0 -> x4, waiting for transfers between devices: none -> 252 us  [ways_resolve(): return jnp.sum(lax.all_gather(row_data, across), 0)]
where the time goes in v1:
time: 920 us; the launch traced here: 911 us
  waiting for transfers between devices  523 us (57%)
  blocking collectives  192 us (21%)
  matrix products  61.3 us (7%)
  other arithmetic  50.6 us (6%)
  starting transfers between devices  36.1 us (4%)
  local copies, waits for them, and re-layouts  33.6 us (4%)
  between operations  14.7 us (2%)
    ppermute x25, waiting for transfers between devices, swapped(): lax.ppermute(x, axis, [(i, i ^ 1 << apart) for i in range(lax.axis_size(a...  260 us
    all_gather x4, waiting for transfers between devices, ways_resolve(): return jnp.sum(lax.all_gather(row_data, across), 0)  252 us
    psum x4, blocking collectives, body(): gram = lax.psum(gram_of(grown), ('gx', 'gy'))  151 us
    psum x1, blocking collectives, body(): lax.psum((local_terms[0], local_terms[1], local_terms[2], local_terms[3])...  40.9 us
    ppermute x25, starting transfers between devices, swapped(): lax.ppermute(x, axis, [(i, i ^ 1 << apart) for i in range(lax.axis_size(a...  33.3 us
    another operation x16, other arithmetic, inverse_factor(): factor = jnp.linalg.cholesky(matrix)  20.4 us
    slice x20, local copies, waits for them, and re-layouts, body(): grown = jnp.where(upper_half, g_real + moved[0], g_imag - moved[1])  18.6 us
  transfers between devices with their start and end apart: 31, of which 30 were waited for; matrix products, arithmetic and copies ran while one was open for 1% of the time, Pallas kernels for 0%

profile of v1, /device:TPU:0, one launch (start us, length us, event | category | flops | bytes accessed | tf_op | source)
XLA Modules:
  0.0 911.5 jit_solution(4932431353959962915)
XLA Ops:
  10.2 2.8 collective-permute-start.1
  14.2 5.4 collective-permute-done.1
  21.4 2.6 fusion.107
  24.0 3.4 collective-permute-done.2
  30.0 4.3 collective-permute-done.3
  34.3 2.3 collective-permute-start.4
  37.7 9.2 %collective-permute-done.4 = f32[1,1,32,2048]{3,2,1,0:T(8,128)S(1)} collective-permute-done((f32[1,1,32,2048]{3,2,1,0:T(8,128)S(1)}, f32[1,1,32,2048]{3,2,1,0:T(8,128)S(1)}, u32[]{:S(2)}, u32[]{:S(2)}) %collective-permute-start.4) | collective-permute-done | bytes 262176 | tf_op jit(solution)/shard_map/ppermute | solution.py:19
  47.3 2.9 fusion.7
  50.2 2.9 select_bitcast_fusion.7
  53.8 62.3 %all-gather.9.cloned.1.call-done = f32[32,32,1024]{2,1,0:T(8,128)} async-done(((f32[1,32,1024]{2,1,0:T(8,128)}), f32[32,32,1024]{2,1,0:T(8,128)}) %all-gather.9.cloned.1.call-update) | async-done | bytes 4194320 | tf_op jit(solution)/shard_map/all_gather | solution.py:12
  116.1 2.4 reduce.20
  118.5 1.9 fusion.52
  120.4 1.9 fusion.51
  122.3 1.9 convolution_subtract_fusion.3
  124.3 1.9 convolution_add_fusion.3
  129.4 12.8 %collective-permute-done.6 = f32[2,1,32,2048]{3,2,1,0:T(8,128)S(1)} collective-permute-done((f32[2,1,32,2048]{3,2,1,0:T(8,128)S(1)}, f32[2,1,32,2048]{3,2,1,0:T(8,128)S(1)}, u32[]{:S(2)}, u32[]{:S(2)}) %collective-permute-start.6) | collective-permute-done | bytes 524320 | tf_op jit(solution)/shard_map/ppermute | solution.py:19
  143.7 11.7 %collective-permute-done.7 = f32[2,1,32,2048]{3,2,1,0:T(8,128)S(1)} collective-permute-done((f32[2,1,32,2048]{3,2,1,0:T(8,128)S(1)}, f32[2,1,32,2048]{3,2,1,0:T(8,128)S(1)}, u32[]{:S(2)}, u32[]{:S(2)}) %collective-permute-start.7) | collective-permute-done | bytes 524320 | tf_op jit(solution)/shard_map/ppermute | solution.py:19
  156.9 10.9 %collective-permute-done.8 = f32[2,1,32,2048]{3,2,1,0:T(8,128)S(1)} collective-permute-done((f32[2,1,32,2048]{3,2,1,0:T(8,128)S(1)}, f32[2,1,32,2048]{3,2,1,0:T(8,128)S(1)}, u32[]{:S(2)}, u32[]{:S(2)}) %collective-permute-start.8) | collective-permute-done | bytes 524320 | tf_op jit(solution)/shard_map/ppermute | solution.py:19
  169.5 22.0 %collective-permute-done.9 = f32[2,1,32,2048]{3,2,1,0:T(8,128)S(1)} collective-permute-done((f32[2,1,32,2048]{3,2,1,0:T(8,128)S(1)}, f32[2,1,32,2048]{3,2,1,0:T(8,128)S(1)}, u32[]{:S(2)}, u32[]{:S(2)}) %collective-permute-start.9) | collective-permute-done | bytes 524320 | tf_op jit(solution)/shard_map/ppermute | solution.py:19
  196.6 2.0 slice.187
  200.3 37.7 %psum.56 = f32[1,32,32]{1,2,0:T(8,128)S(1)} all-reduce(f32[1,32,32]{1,2,0:T(8,128)S(1)} %convolution_bitcast_fusion.10), channel_id=1, replica_groups=mesh['gx'=8,'gy'=4] {'gx','gy'}, use_global_device_ids=true, to_apply=%region_1.2 | all-reduce | flops 1024 | bytes 8192 | tf_op jit(solution)/shard_map/psum | solution.py:126
  238.0 2.9 custom-call.21
  242.3 2.4 custom-call.22
  250.8 63.1 %all-gather.11.cloned.1.call-done = f32[32,32,1024]{2,1,0:T(8,128)} async-done(((f32[1,32,1024]{2,1,0:T(8,128)}), f32[32,32,1024]{2,1,0:T(8,128)}) %all-gather.11.cloned.1.call-update) | async-done | bytes 4194320 | tf_op jit(solution)/shard_map/all_gather | solution.py:12
  313.9 2.4 reduce.21
  316.4 1.9 fusion.54
  320.2 1.9 convolution_subtract_fusion.2
  322.1 1.9 convolution_add_fusion.2
  327.3 12.8 %collective-permute-done.11 = f32[2,1,32,2048]{3,2,1,0:T(8,128)S(1)} collective-permute-done((f32[2,1,32,2048]{3,2,1,0:T(8,128)S(1)}, f32[2,1,32,2048]{3,2,1,0:T(8,128)S(1)}, u32[]{:S(2)}, u32[]{:S(2)}) %collective-permute-start.11) | collective-permute-done | bytes 524320 | tf_op jit(solution)/shard_map/ppermute | solution.py:19
  341.6 11.7 %collective-permute-done.12 = f32[2,1,32,2048]{3,2,1,0:T(8,128)S(1)} collective-permute-done((f32[2,1,32,2048]{3,2,1,0:T(8,128)S(1)}, f32[2,1,32,2048]{3,2,1,0:T(8,128)S(1)}, u32[]{:S(2)}, u32[]{:S(2)}) %collective-permute-start.12) | collective-permute-done | bytes 524320 | tf_op jit(solution)/shard_map/ppermute | solution.py:19
  354.7 10.9 %collective-permute-done.13 = f32[2,1,32,2048]{3,2,1,0:T(8,128)S(1)} collective-permute-done((f32[2,1,32,2048]{3,2,1,0:T(8,128)S(1)}, f32[2,1,32,2048]{3,2,1,0:T(8,128)S(1)}, u32[]{:S(2)}, u32[]{:S(2)}) %collective-permute-start.13) | collective-permute-done | bytes 524320 | tf_op jit(solution)/shard_map/ppermute | solution.py:19
  367.3 22.0 %collective-permute-done.14 = f32[2,1,32,2048]{3,2,1,0:T(8,128)S(1)} collective-permute-done((f32[2,1,32,2048]{3,2,1,0:T(8,128)S(1)}, f32[2,1,32,2048]{3,2,1,0:T(8,128)S(1)}, u32[]{:S(2)}, u32[]{:S(2)}) %collective-permute-start.14) | collective-permute-done | bytes 524320 | tf_op jit(solution)/shard_map/ppermute | solution.py:19
  394.4 2.0 slice.195
  398.1 37.7 %psum.57 = f32[1,32,32]{1,2,0:T(8,128)S(1)} all-reduce(f32[1,32,32]{1,2,0:T(8,128)S(1)} %convolution_bitcast_fusion.9), channel_id=1, replica_groups=mesh['gx'=8,'gy'=4] {'gx','gy'}, use_global_device_ids=true, to_apply=%region_5.8 | all-reduce | flops 1024 | bytes 8192 | tf_op jit(solution)/shard_map/psum | solution.py:126
  435.9 2.9 custom-call.23
  440.2 2.4 custom-call.24
  448.7 63.1 %all-gather.13.cloned.1.call-done = f32[32,32,1024]{2,1,0:T(8,128)} async-done(((f32[1,32,1024]{2,1,0:T(8,128)}), f32[32,32,1024]{2,1,0:T(8,128)}) %all-gather.13.cloned.1.call-update) | async-done | bytes 4194320 | tf_op jit(solution)/shard_map/all_gather | solution.py:12
  511.8 2.4 reduce.22
  518.0 1.9 convolution_subtract_fusion.1
  519.9 1.9 convolution_add_fusion.1
  525.1 12.8 %collective-permute-done.16 = f32[2,1,32,2048]{3,2,1,0:T(8,128)S(1)} collective-permute-done((f32[2,1,32,2048]{3,2,1,0:T(8,128)S(1)}, f32[2,1,32,2048]{3,2,1,0:T(8,128)S(1)}, u32[]{:S(2)}, u32[]{:S(2)}) %collective-permute-start.16) | collective-permute-done | bytes 524320 | tf_op jit(solution)/shard_map/ppermute | solution.py:19
  539.4 11.7 %collective-permute-done.17 = f32[2,1,32,2048]{3,2,1,0:T(8,128)S(1)} collective-permute-done((f32[2,1,32,2048]{3,2,1,0:T(8,128)S(1)}, f32[2,1,32,2048]{3,2,1,0:T(8,128)S(1)}, u32[]{:S(2)}, u32[]{:S(2)}) %collective-permute-start.17) | collective-permute-done | bytes 524320 | tf_op jit(solution)/shard_map/ppermute | solution.py:19
  552.6 10.9 %collective-permute-done.18 = f32[2,1,32,2048]{3,2,1,0:T(8,128)S(1)} collective-permute-done((f32[2,1,32,2048]{3,2,1,0:T(8,128)S(1)}, f32[2,1,32,2048]{3,2,1,0:T(8,128)S(1)}, u32[]{:S(2)}, u32[]{:S(2)}) %collective-permute-start.18) | collective-permute-done | bytes 524320 | tf_op jit(solution)/shard_map/ppermute | solution.py:19
  565.1 22.0 %collective-permute-done.19 = f32[2,1,32,2048]{3,2,1,0:T(8,128)S(1)} collective-permute-done((f32[2,1,32,2048]{3,2,1,0:T(8,128)S(1)}, f32[2,1,32,2048]{3,2,1,0:T(8,128)S(1)}, u32[]{:S(2)}, u32[]{:S(2)}) %collective-permute-start.19) | collective-permute-done | bytes 524320 | tf_op jit(solution)/shard_map/ppermute | solution.py:19
  592.3 2.0 slice.203
  596.0 37.9 %psum.58 = f32[1,32,32]{1,2,0:T(8,128)S(1)} all-reduce(f32[1,32,32]{1,2,0:T(8,128)S(1)} %convolution_bitcast_fusion.8), channel_id=1, replica_groups=mesh['gx'=8,'gy'=4] {'gx','gy'}, use_global_device_ids=true, to_apply=%region_7.10 | all-reduce | flops 1024 | bytes 8192 | tf_op jit(solution)/shard_map/psum | solution.py:126
  634.0 2.9 custom-call.25
  638.2 2.4 custom-call.26
  646.7 63.1 %all-gather.15.cloned.1.call-done = f32[32,32,1024]{2,1,0:T(8,128)} async-done(((f32[1,32,1024]{2,1,0:T(8,128)}), f32[32,32,1024]{2,1,0:T(8,128)}) %all-gather.15.cloned.1.call-update) | async-done | bytes 4194320 | tf_op jit(solution)/shard_map/all_gather | solution.py:12
  709.8 2.4 reduce.23
  714.2 1.9 fusion.57
  716.1 1.9 convolution_subtract_fusion
  718.0 1.9 convolution_add_fusion
  723.1 12.8 %collective-permute-done.21 = f32[2,1,32,2048]{3,2,1,0:T(8,128)S(1)} collective-permute-done((f32[2,1,32,2048]{3,2,1,0:T(8,128)S(1)}, f32[2,1,32,2048]{3,2,1,0:T(8,128)S(1)}, u32[]{:S(2)}, u32[]{:S(2)}) %collective-permute-start.21) | collective-permute-done | bytes 524320 | tf_op jit(solution)/shard_map/ppermute | solution.py:19
  737.4 11.7 %collective-permute-done.22 = f32[2,1,32,2048]{3,2,1,0:T(8,128)S(1)} collective-permute-done((f32[2,1,32,2048]{3,2,1,0:T(8,128)S(1)}, f32[2,1,32,2048]{3,2,1,0:T(8,128)S(1)}, u32[]{:S(2)}, u32[]{:S(2)}) %collective-permute-start.22) | collective-permute-done | bytes 524320 | tf_op jit(solution)/shard_map/ppermute | solution.py:19
  750.6 10.9 %collective-permute-done.23 = f32[2,1,32,2048]{3,2,1,0:T(8,128)S(1)} collective-permute-done((f32[2,1,32,2048]{3,2,1,0:T(8,128)S(1)}, f32[2,1,32,2048]{3,2,1,0:T(8,128)S(1)}, u32[]{:S(2)}, u32[]{:S(2)}) %collective-permute-start.23) | collective-permute-done | bytes 524320 | tf_op jit(solution)/shard_map/ppermute | solution.py:19
  763.2 22.0 %collective-permute-done.24 = f32[2,1,32,2048]{3,2,1,0:T(8,128)S(1)} collective-permute-done((f32[2,1,32,2048]{3,2,1,0:T(8,128)S(1)}, f32[2,1,32,2048]{3,2,1,0:T(8,128)S(1)}, u32[]{:S(2)}, u32[]{:S(2)}) %collective-permute-start.24) | collective-permute-done | bytes 524320 | tf_op jit(solution)/shard_map/ppermute | solution.py:19
  787.1 37.7 %psum.59 = f32[1,32,32]{1,2,0:T(8,128)S(1)} all-reduce(f32[1,32,32]{1,2,0:T(8,128)S(1)} %convolution_bitcast_fusion.7), channel_id=1, replica_groups=mesh['gx'=8,'gy'=4] {'gx','gy'}, use_global_device_ids=true, to_apply=%region_9.12 | all-reduce | flops 1024 | bytes 8192 | tf_op jit(solution)/shard_map/psum | solution.py:126
  824.9 2.9 custom-call.27
  829.1 2.4 custom-call.28
  836.4 11.6 %collective-permute-done.26 = f32[1,32,32,1]{3,1,2,0:T(8,128)S(1)} collective-permute-done((f32[1,32,32,1]{3,1,2,0:T(8,128)S(1)}, f32[1,32,32,1]{3,1,2,0:T(8,128)S(1)}, u32[]{:S(2)}, u32[]{:S(2)}) %collective-permute-start.26) | collective-permute-done | bytes 4128 | tf_op jit(solution)/shard_map/ppermute | solution.py:25
  851.4 40.9 %all-reduce = (f32[1,1,32,32]{2,3,1,0:T(8,128)S(1)}, f32[1,1,32,32]{2,3,1,0:T(8,128)S(1)}, f32[1,1,32,32]{3,2,1,0:T(8,128)S(1)}, f32[1,1,32,32]{3,2,1,0:T(8,128)S(1)}) all-reduce(f32[1,1,32,32]{2,3,1,0:T(8,128)S(1)} %convolution_bitcast_fusion.5, ...), channel_id=1, replica_groups=mesh['gx'=8,'gy'=4] {'gx','gy'}, use_global_device_ids=true, to_apply=%region_10.13 | all-reduce | flops 4096 | bytes 32768 | tf_op jit(solution)/shard_map/psum | solution.py:132
  892.5 5.9 custom-call.13
  898.6 4.9 custom-call.14
  (171 shorter events, 105.1 us)
Async XLA Ops:
  7.2 108.9 %all-gather.9.cloned.1.call-start = ((), (), s32[]{:S(2)}) async-start(), calls=%async_computation | async-start | bytes 4325376 | tf_op jit(solution)/shard_map/all_gather | solution.py:12
  8.4 1.7 collective-permute-start
  10.2 9.5 %collective-permute-start.1 = (f32[1,1,32,2048]{3,2,1,0:T(8,128)S(1)}, f32[1,1,32,2048]{3,2,1,0:T(8,128)S(1)}, u32[]{:S(2)}, u32[]{:S(2)}) collective-permute-start(f32[1,1,32,2048]{3,2,1,0:T(8,128)S(1)} %collective-permute-done), channel_id=1, source_target_pairs={{0,8},{4,12},{8,0},{12,4},{16,24},{20,28},{24,16},{28,20},{1,9},{5... | collective-permute-start | bytes 786440 | tf_op jit(solution)/shard_map/ppermute | solution.py:19
  19.6 7.8 collective-permute-start.2
  24.0 13.7 %copy-start = (bf16[1,1,32,64,512]{4,3,2,1,0:T(8,128)(2,1)}, bf16[1,1,32,64,512]{4,3,2,1,0:T(8,128)(2,1)S(1)}, u32[]{:S(2)}) copy-start(bf16[1,1,32,64,512]{4,3,2,1,0:T(8,128)(2,1)S(1)} %get-tuple-element.17) | copy-start | bytes 6291460
  27.4 6.9 collective-permute-start.3
  34.3 12.6 %collective-permute-start.4 = (f32[1,1,32,2048]{3,2,1,0:T(8,128)S(1)}, f32[1,1,32,2048]{3,2,1,0:T(8,128)S(1)}, u32[]{:S(2)}, u32[]{:S(2)}) collective-permute-start(f32[1,1,32,2048]{3,2,1,0:T(8,128)S(1)} %collective-permute-done.3), channel_id=1, source_target_pairs={{0,2},{1,3},{2,0},{3,1},{4,6},{5,7},{6,4},{7,5},{8,10},{9,11},{10,... | collective-permute-start | bytes 786440 | tf_op jit(solution)/shard_map/ppermute | solution.py:19
  53.8 260.2 %all-gather.11.cloned.1.call-start = ((), (), s32[]{:S(2)}) async-start(), calls=%async_computation.1 | async-start | bytes 4325376 | tf_op jit(solution)/shard_map/all_gather | solution.py:12
  118.5 1.9 copy-start.1
  126.2 2.0 collective-permute-start.5
  128.2 14.1 %collective-permute-start.6 = (f32[2,1,32,2048]{3,2,1,0:T(8,128)S(1)}, f32[2,1,32,2048]{3,2,1,0:T(8,128)S(1)}, u32[]{:S(2)}, u32[]{:S(2)}) collective-permute-start(f32[2,1,32,2048]{3,2,1,0:T(8,128)S(1)} %collective-permute-done.5), channel_id=1, source_target_pairs={{0,8},{4,12},{8,0},{12,4},{16,24},{20,28},{24,16},{28,20},{1,9},{5... | collective-permute-start | bytes 1572872 | tf_op jit(solution)/shard_map/ppermute | solution.py:19
  142.3 13.2 %collective-permute-start.7 = (f32[2,1,32,2048]{3,2,1,0:T(8,128)S(1)}, f32[2,1,32,2048]{3,2,1,0:T(8,128)S(1)}, u32[]{:S(2)}, u32[]{:S(2)}) collective-permute-start(f32[2,1,32,2048]{3,2,1,0:T(8,128)S(1)} %collective-permute-done.6), channel_id=1, source_target_pairs={{0,16},{4,20},{8,24},{12,28},{16,0},{20,4},{24,8},{28,12},{1,17},{... | collective-permute-start | bytes 1572872 | tf_op jit(solution)/shard_map/ppermute | solution.py:19
  155.5 12.4 %collective-permute-start.8 = (f32[2,1,32,2048]{3,2,1,0:T(8,128)S(1)}, f32[2,1,32,2048]{3,2,1,0:T(8,128)S(1)}, u32[]{:S(2)}, u32[]{:S(2)}) collective-permute-start(f32[2,1,32,2048]{3,2,1,0:T(8,128)S(1)} %collective-permute-done.7), channel_id=1, source_target_pairs={{0,1},{1,0},{2,3},{3,2},{4,5},{5,4},{6,7},{7,6},{8,9},{9,8},{10,11... | collective-permute-start | bytes 1572872 | tf_op jit(solution)/shard_map/ppermute | solution.py:19
  167.8 23.6 %collective-permute-start.9 = (f32[2,1,32,2048]{3,2,1,0:T(8,128)S(1)}, f32[2,1,32,2048]{3,2,1,0:T(8,128)S(1)}, u32[]{:S(2)}, u32[]{:S(2)}) collective-permute-start(f32[2,1,32,2048]{3,2,1,0:T(8,128)S(1)} %collective-permute-done.8), channel_id=1, source_target_pairs={{0,2},{1,3},{2,0},{3,1},{4,6},{5,7},{6,4},{7,5},{8,10},{9,11},{10,... | collective-permute-start | bytes 1572872 | tf_op jit(solution)/shard_map/ppermute | solution.py:19
  245.0 1.8 copy-start.2
  250.8 261.0 %all-gather.13.cloned.1.call-start = ((), (), s32[]{:S(2)}) async-start(), calls=%async_computation.2 | async-start | bytes 4325376 | tf_op jit(solution)/shard_map/all_gather | solution.py:12
  316.4 1.9 copy-start.3
  324.0 2.0 collective-permute-start.10
  326.0 14.1 %collective-permute-start.11 = (f32[2,1,32,2048]{3,2,1,0:T(8,128)S(1)}, f32[2,1,32,2048]{3,2,1,0:T(8,128)S(1)}, u32[]{:S(2)}, u32[]{:S(2)}) collective-permute-start(f32[2,1,32,2048]{3,2,1,0:T(8,128)S(1)} %collective-permute-done.10), channel_id=1, source_target_pairs={{0,8},{4,12},{8,0},{12,4},{16,24},{20,28},{24,16},{28,20},{1,9},{5... | collective-permute-start | bytes 1572872 | tf_op jit(solution)/shard_map/ppermute | solution.py:19
  340.1 13.2 %collective-permute-start.12 = (f32[2,1,32,2048]{3,2,1,0:T(8,128)S(1)}, f32[2,1,32,2048]{3,2,1,0:T(8,128)S(1)}, u32[]{:S(2)}, u32[]{:S(2)}) collective-permute-start(f32[2,1,32,2048]{3,2,1,0:T(8,128)S(1)} %collective-permute-done.11), channel_id=1, source_target_pairs={{0,16},{4,20},{8,24},{12,28},{16,0},{20,4},{24,8},{28,12},{1,17},{... | collective-permute-start | bytes 1572872 | tf_op jit(solution)/shard_map/ppermute | solution.py:19
  353.3 12.4 %collective-permute-start.13 = (f32[2,1,32,2048]{3,2,1,0:T(8,128)S(1)}, f32[2,1,32,2048]{3,2,1,0:T(8,128)S(1)}, u32[]{:S(2)}, u32[]{:S(2)}) collective-permute-start(f32[2,1,32,2048]{3,2,1,0:T(8,128)S(1)} %collective-permute-done.12), channel_id=1, source_target_pairs={{0,1},{1,0},{2,3},{3,2},{4,5},{5,4},{6,7},{7,6},{8,9},{9,8},{10,11... | collective-permute-start | bytes 1572872 | tf_op jit(solution)/shard_map/ppermute | solution.py:19
  365.7 23.6 %collective-permute-start.14 = (f32[2,1,32,2048]{3,2,1,0:T(8,128)S(1)}, f32[2,1,32,2048]{3,2,1,0:T(8,128)S(1)}, u32[]{:S(2)}, u32[]{:S(2)}) collective-permute-start(f32[2,1,32,2048]{3,2,1,0:T(8,128)S(1)} %collective-permute-done.13), channel_id=1, source_target_pairs={{0,2},{1,3},{2,0},{3,1},{4,6},{5,7},{6,4},{7,5},{8,10},{9,11},{10,... | collective-permute-start | bytes 1572872 | tf_op jit(solution)/shard_map/ppermute | solution.py:19
  442.9 1.8 copy-start.4
  448.7 261.1 %all-gather.15.cloned.1.call-start = ((), (), s32[]{:S(2)}) async-start(), calls=%async_computation.3 | async-start | bytes 4325376 | tf_op jit(solution)/shard_map/all_gather | solution.py:12
  514.2 1.9 copy-start.5
  521.9 2.0 collective-permute-start.15
  523.8 14.1 %collective-permute-start.16 = (f32[2,1,32,2048]{3,2,1,0:T(8,128)S(1)}, f32[2,1,32,2048]{3,2,1,0:T(8,128)S(1)}, u32[]{:S(2)}, u32[]{:S(2)}) collective-permute-start(f32[2,1,32,2048]{3,2,1,0:T(8,128)S(1)} %collective-permute-done.15), channel_id=1, source_target_pairs={{0,8},{4,12},{8,0},{12,4},{16,24},{20,28},{24,16},{28,20},{1,9},{5... | collective-permute-start | bytes 1572872 | tf_op jit(solution)/shard_map/ppermute | solution.py:19
  537.9 13.2 %collective-permute-start.17 = (f32[2,1,32,2048]{3,2,1,0:T(8,128)S(1)}, f32[2,1,32,2048]{3,2,1,0:T(8,128)S(1)}, u32[]{:S(2)}, u32[]{:S(2)}) collective-permute-start(f32[2,1,32,2048]{3,2,1,0:T(8,128)S(1)} %collective-permute-done.16), channel_id=1, source_target_pairs={{0,16},{4,20},{8,24},{12,28},{16,0},{20,4},{24,8},{28,12},{1,17},{... | collective-permute-start | bytes 1572872 | tf_op jit(solution)/shard_map/ppermute | solution.py:19
  551.1 12.4 %collective-permute-start.18 = (f32[2,1,32,2048]{3,2,1,0:T(8,128)S(1)}, f32[2,1,32,2048]{3,2,1,0:T(8,128)S(1)}, u32[]{:S(2)}, u32[]{:S(2)}) collective-permute-start(f32[2,1,32,2048]{3,2,1,0:T(8,128)S(1)} %collective-permute-done.17), channel_id=1, source_target_pairs={{0,1},{1,0},{2,3},{3,2},{4,5},{5,4},{6,7},{7,6},{8,9},{9,8},{10,11... | collective-permute-start | bytes 1572872 | tf_op jit(solution)/shard_map/ppermute | solution.py:19
  563.5 23.6 %collective-permute-start.19 = (f32[2,1,32,2048]{3,2,1,0:T(8,128)S(1)}, f32[2,1,32,2048]{3,2,1,0:T(8,128)S(1)}, u32[]{:S(2)}, u32[]{:S(2)}) collective-permute-start(f32[2,1,32,2048]{3,2,1,0:T(8,128)S(1)} %collective-permute-done.18), channel_id=1, source_target_pairs={{0,2},{1,3},{2,0},{3,1},{4,6},{5,7},{6,4},{7,5},{8,10},{9,11},{10,... | collective-permute-start | bytes 1572872 | tf_op jit(solution)/shard_map/ppermute | solution.py:19
  640.9 1.8 copy-start.6
  712.2 1.9 copy-start.7
  719.9 2.0 collective-permute-start.20
  721.9 14.1 %collective-permute-start.21 = (f32[2,1,32,2048]{3,2,1,0:T(8,128)S(1)}, f32[2,1,32,2048]{3,2,1,0:T(8,128)S(1)}, u32[]{:S(2)}, u32[]{:S(2)}) collective-permute-start(f32[2,1,32,2048]{3,2,1,0:T(8,128)S(1)} %collective-permute-done.20), channel_id=1, source_target_pairs={{0,8},{4,12},{8,0},{12,4},{16,24},{20,28},{24,16},{28,20},{1,9},{5... | collective-permute-start | bytes 1572872 | tf_op jit(solution)/shard_map/ppermute | solution.py:19
  736.0 13.2 %collective-permute-start.22 = (f32[2,1,32,2048]{3,2,1,0:T(8,128)S(1)}, f32[2,1,32,2048]{3,2,1,0:T(8,128)S(1)}, u32[]{:S(2)}, u32[]{:S(2)}) collective-permute-start(f32[2,1,32,2048]{3,2,1,0:T(8,128)S(1)} %collective-permute-done.21), channel_id=1, source_target_pairs={{0,16},{4,20},{8,24},{12,28},{16,0},{20,4},{24,8},{28,12},{1,17},{... | collective-permute-start | bytes 1572872 | tf_op jit(solution)/shard_map/ppermute | solution.py:19
  749.2 12.4 %collective-permute-start.23 = (f32[2,1,32,2048]{3,2,1,0:T(8,128)S(1)}, f32[2,1,32,2048]{3,2,1,0:T(8,128)S(1)}, u32[]{:S(2)}, u32[]{:S(2)}) collective-permute-start(f32[2,1,32,2048]{3,2,1,0:T(8,128)S(1)} %collective-permute-done.22), channel_id=1, source_target_pairs={{0,1},{1,0},{2,3},{3,2},{4,5},{5,4},{6,7},{7,6},{8,9},{9,8},{10,11... | collective-permute-start | bytes 1572872 | tf_op jit(solution)/shard_map/ppermute | solution.py:19
  761.5 23.6 %collective-permute-start.24 = (f32[2,1,32,2048]{3,2,1,0:T(8,128)S(1)}, f32[2,1,32,2048]{3,2,1,0:T(8,128)S(1)}, u32[]{:S(2)}, u32[]{:S(2)}) collective-permute-start(f32[2,1,32,2048]{3,2,1,0:T(8,128)S(1)} %collective-permute-done.23), channel_id=1, source_target_pairs={{0,2},{1,3},{2,0},{3,1},{4,6},{5,7},{6,4},{7,5},{8,10},{9,11},{10,... | collective-permute-start | bytes 1572872 | tf_op jit(solution)/shard_map/ppermute | solution.py:19
  832.7 15.3 %collective-permute-start.26 = (f32[1,32,32,1]{3,1,2,0:T(8,128)S(1)}, f32[1,32,32,1]{3,1,2,0:T(8,128)S(1)}, u32[]{:S(2)}, u32[]{:S(2)}) collective-permute-start(f32[1,32,32,1]{3,1,2,0:T(8,128)S(1)} %bitcast.342), channel_id=1, source_target_pairs={{1,0},{2,1},{3,2},{5,4},{6,5},{7,6},{9,8},{10,9},{11,10},{13,12},{... | collective-permute-start | bytes 12296 | tf_op jit(solution)/shard_map/ppermute | solution.py:25
  835.1 14.9 %collective-permute-start.25 = (f32[1,32,1,64]{3,1,2,0:T(8,128)S(1)}, f32[1,32,1,64]{3,1,2,0:T(8,128)S(1)}, u32[]{:S(2)}, u32[]{:S(2)}) collective-permute-start(f32[1,32,1,64]{3,1,2,0:T(8,128)S(1)} %slice.232), channel_id=1, source_target_pairs={{4,0},{8,4},{12,8},{16,12},{20,16},{24,20},{28,24},{5,1},{9,5},{13... | collective-permute-start | bytes 24584 | tf_op jit(solution)/shard_map/ppermute | solution.py:25
Sparse Core Ops, SparseCore 0:
  53.9 62.1 all-gather.8
  250.9 62.9 all-gather.10
  448.8 62.9 all-gather.12
  646.8 62.9 all-gather.14
